TPU v7x, 32 devices: a whole 2x2x4 slice. The times are simulated.
32 devices in a mesh: node: 8 (over y, x, core), chip: 4 (over z).
Axes of the slice: x: 2, y: 2, z: 4, core: 2. Of those that a mesh axis runs over, the one named last changes fastest.
Arguments:
- momentum: float32 [32, 128, 512], P(('node', 'chip')), may hold values from -6 to 6
- gradient: bfloat16 [32, 128, 512], P(('node', 'chip')), may hold values from -6 to 6
- indices: int32 [32, 16, 32], P(('node', 'chip')), may hold values from 0 to 4095, as said below
Outputs:
- new_momentum: float32 [32, 128, 512], P(('node', 'chip'))
- update: float32 [128, 512], replicated
Inputs may be any that keep to these rules, and one draw needn't show every extreme that they name: `indices`: the 32 entries of each row name distinct coefficients of their span, coefficient (k, l) being k * 64 + l.
All inputs are finite; a program needn't handle non-finite values.
Results may differ from a plain program's by a relative error of at most 0.0029.
Values may be sent and summed in bfloat16 or wider, within the bound.
A program may use at most 64 MiB of HBM per device.

v0:
```python
import math
import jax
import jax.numpy as jnp
from jax import lax
from jax.sharding import PartitionSpec as P

SPAN = 64


def dct_table(edge_len):
    orders = jnp.arange(edge_len, dtype=jnp.float32)
    wave_no = orders[:, None]
    cell_no = orders[None, :]
    factor = jnp.where(wave_no == 0.0, math.sqrt(1.0 / edge_len), math.sqrt(2.0 / edge_len))
    return factor * jnp.cos(math.pi * (2.0 * cell_no + 1.0) * wave_no / (2.0 * edge_len))


def forward(grid_field, cosines, edge_len):
    row_blocks = grid_field.shape[0] // edge_len
    col_blocks = grid_field.shape[1] // edge_len
    blocks = grid_field.reshape(row_blocks, edge_len, col_blocks, edge_len).transpose(0, 2, 1, 3)
    coeffs = jnp.einsum(
        "kn,abnm,lm->abkl", cosines, blocks, cosines, precision=lax.Precision.HIGHEST
    )
    return coeffs.reshape(row_blocks * col_blocks, edge_len * edge_len)


def inverse_blocks(coeffs, cosines, edge_len):
    blocks = coeffs.reshape(coeffs.shape[0], edge_len, edge_len)
    return jnp.einsum("kn,ckl,lm->cnm", cosines, blocks, cosines, precision=lax.Precision.HIGHEST)


def place_blocks(blocks, row_count, col_count, edge_len):
    shaped = blocks.reshape(row_count // edge_len, col_count // edge_len, edge_len, edge_len)
    return shaped.transpose(0, 2, 1, 3).reshape(row_count, col_count)


def normalized(blocks):
    energy = jnp.mean(blocks * blocks, axis=(1, 2), keepdims=True)
    return blocks / jnp.sqrt(energy + 1.0)


def decode_block(picked, slots):
    n_spans = picked.shape[1]
    values_rows = jnp.moveaxis(picked, 1, 0).reshape(n_spans, -1)
    slot_rows = jnp.moveaxis(slots, 1, 0).reshape(n_spans, -1)
    orders = jnp.arange(SPAN, dtype=jnp.int32)[None, :]

    def one_span(pair):
        vals, where = pair
        wave_rows = (where // SPAN)[:, None] == orders
        wave_cols = (where % SPAN)[:, None] == orders
        left_hot = wave_rows.astype(jnp.bfloat16)
        right_hot = jnp.where(wave_cols, vals[:, None], jnp.zeros((), jnp.bfloat16))
        block = lax.dot_general(
            left_hot, right_hot, (((0,), (0,)), ((), ())), preferred_element_type=jnp.float32
        )
        return block.reshape(SPAN * SPAN)

    return lax.map(one_span, (values_rows, slot_rows))


def decode_lists(totals, picked, slots):
    count = picked.shape[0]
    group_len = 1
    for trial in range(1, 17):
        if count % trial == 0:
            group_len = trial
    picked_groups = picked.reshape((count // group_len, group_len) + picked.shape[1:])
    slot_groups = slots.reshape((count // group_len, group_len) + slots.shape[1:])

    def add_group(step, carry):
        return carry + decode_block(picked_groups[step], slot_groups[step])

    return lax.fori_loop(0, count // group_len, add_group, totals)


def shards(momentum, gradient, indices):
    cosines = dct_table(SPAN)
    row_count = momentum.shape[1]
    col_count = momentum.shape[2]
    blended = 0.9 * momentum[0] + gradient[0].astype(jnp.float32)
    coeffs = forward(blended, cosines, SPAN)
    slots = indices[0]
    picked = jnp.take_along_axis(coeffs, slots, axis=1).astype(jnp.bfloat16)
    sparse = decode_block(picked[None], indices)
    own_part = place_blocks(inverse_blocks(sparse, cosines, SPAN), row_count, col_count, SPAN)
    new_momentum = (blended - own_part)[None]
    partial_sum = decode_lists(
        jnp.zeros_like(coeffs),
        lax.all_gather(picked[None], "chip", axis=0, tiled=True),
        lax.all_gather(indices, "chip", axis=0, tiled=True),
    )
    totals = lax.psum(partial_sum, "node")
    update = place_blocks(
        normalized(inverse_blocks(totals, cosines, SPAN)), row_count, col_count, SPAN
    )
    return (new_momentum, update)


def solution(mesh):
    return jax.shard_map(
        shards,
        mesh=mesh,
        in_specs=(
            P(("node", "chip"), None, None),
            P(("node", "chip"), None, None),
            P(("node", "chip"), None, None),
        ),
        out_specs=(P(("node", "chip"), None, None), P()),
        check_vma=False,
    )
```

profile of v0, /device:TPU:0, one launch (start us, length us, event | category | flops | bytes accessed | tf_op | source)
XLA Modules:
  0.0 127.8 jit_solution(4356147614158876346)
XLA Ops:
  7.2 0.8 fusion.53
  8.0 14.8 %all_gather.6 = s32[4,16,32]{2,1,0:T(8,128)S(1)} all-gather(s32[1,16,32]{2,1,0:T(8,128)S(1)} %copy-done), channel_id=1, replica_groups=mesh['node'=8,'chip'=4] {'chip'}, dimensions={0}, use_global_device_ids=true | all-gather | bytes 10240 | tf_op jit(solution)/shard_map/all_gather | solution.py:92
  22.8 1.1 convert_add_fusion
  24.3 1.7 %fusion.20 = f32[2,8,64,64]{2,3,1,0:T(8,128)S(1)} fusion(f32[2,64,8,64]{1,3,2,0:T(8,128)S(1)} %copy.20, f32[64]{0:T(128)S(1)} %get-tuple-element.232, f32[64]{0:T(128)S(1)} %get-tuple-element.231), kind=kOutput, calls=%fused_computation.37 | convolution fusion | flops 50343936 | bytes 524800 | tf_op jit(solution)/shard_map/kn,abnm,lm->abkl/dot_general | solution.py:22
  26.0 0.7 fusion.22
  26.7 0.3 reshape.216
  27.0 4.8 %gather_fusion = bf16[512]{0:T(512)(128)(2,1)S(1)} fusion(bf16[16,4096]{1,0:T(8,128)(2,1)S(1)} %reshape.216, s32[512]{0:T(512)S(1)} %reshape.225), kind=kCustom, calls=%fused_computation | custom fusion | bytes 6144 | tf_op jit(solution)/shard_map/jit(take_along_axis)/gather | solution.py:85
  32.0 13.2 %all_gather.7 = bf16[4,16,32]{2,1,0:T(8,128)(2,1)S(1)} all-gather(bf16[1,16,32]{2,1,0:T(8,128)(2,1)S(1)} %select_convert_fusion), channel_id=1, replica_groups=mesh['node'=8,'chip'=4] {'chip'}, dimensions={0}, use_global_device_ids=true | all-gather | bytes 5120 | tf_op jit(solution)/shard_map/all_gather | solution.py:91
  45.4 13.3 %while.37 = (s32[]{:T(128)}, f32[16,4096]{1,0:T(8,128)S(1)}, s32[16,128]{1,0:T(8,128)S(1)}, bf16[16,128]{1,0:T(8,128)(2,1)S(1)}, s32[]{:T(128)}, /*index=5*/s32[]{:T(128)}) while((s32[]{:T(128)}, f32[16,4096]{1,0:T(8,128)S(1)}, s32[16,128]{1,0:T(8,128)S(1)}, bf16[16,128]{1,0:T(8,128)(2,1)S(1)}, s32[]{:T(128)}, ...), condition=%wide.region_3.4_spmd.clone.clone, body=%wide.region_2.3_spmd.clone.clone.sunk | while | flops 1075714 | bytes 86353 | solution.py:60
  45.5 0.3 fusion.72
  45.8 0.4 dynamic_update_slice.20
  46.3 0.3 fusion.72
  46.7 0.4 dynamic_update_slice.20
  47.1 0.3 fusion.72
  47.5 0.4 dynamic_update_slice.20
  48.0 0.3 fusion.72
  48.3 0.4 dynamic_update_slice.20
  48.8 0.3 fusion.72
  49.2 0.4 dynamic_update_slice.20
  49.6 0.3 fusion.72
  50.0 0.4 dynamic_update_slice.20
  50.8 0.4 dynamic_update_slice.20
  51.3 0.3 fusion.72
  51.7 0.4 dynamic_update_slice.20
  52.1 0.3 fusion.72
  52.5 0.4 dynamic_update_slice.20
  53.0 0.3 fusion.72
  53.3 0.4 dynamic_update_slice.20
  54.1 0.4 dynamic_update_slice.20
  54.6 0.3 fusion.72
  55.0 0.4 dynamic_update_slice.20
  55.5 0.3 fusion.72
  55.8 0.4 dynamic_update_slice.20
  56.3 0.3 fusion.72
  56.6 0.4 dynamic_update_slice.20
  57.5 0.4 dynamic_update_slice.20
  58.3 0.4 dynamic_update_slice.20
  58.9 1.0 copy.27
  60.1 13.3 %while.36 = (s32[]{:T(128)}, f32[16,4096]{1,0:T(8,128)S(1)}, s32[16,32]{1,0:T(8,128)S(1)}, bf16[16,32]{1,0:T(8,128)(2,1)S(1)}, s32[]{:T(128)}, /*index=5*/s32[]{:T(128)}) while((s32[]{:T(128)}, f32[16,4096]{1,0:T(8,128)S(1)}, s32[16,32]{1,0:T(8,128)S(1)}, bf16[16,32]{1,0:T(8,128)(2,1)S(1)}, s32[]{:T(128)}, ...), condition=%wide.region_1.2_spmd.clone.clone, body=%wide.region_0.1_spmd.clone.clone.sunk | while | flops 268930 | bytes 83089 | solution.py:60
  60.5 0.4 dynamic_update_slice.19
  61.3 0.4 dynamic_update_slice.19
  62.2 0.4 dynamic_update_slice.19
  63.0 0.4 dynamic_update_slice.19
  63.8 0.4 dynamic_update_slice.19
  64.7 0.4 dynamic_update_slice.19
  65.5 0.4 dynamic_update_slice.19
  66.3 0.4 dynamic_update_slice.19
  67.2 0.4 dynamic_update_slice.19
  68.0 0.4 dynamic_update_slice.19
  68.8 0.4 dynamic_update_slice.19
  69.7 0.4 dynamic_update_slice.19
  70.5 0.4 dynamic_update_slice.19
  71.3 0.4 dynamic_update_slice.19
  72.2 0.4 dynamic_update_slice.19
  73.0 0.4 dynamic_update_slice.19
  73.6 0.7 fusion.31
  74.4 0.7 fusion.29
  75.1 0.3 copy.24
  75.5 0.7 sub.16
  76.3 39.7 %all-reduce.2.cloned.1.call-done = f32[16,64,64]{1,2,0:T(8,128)} async-done(((f32[16,64,64]{1,2,0:T(8,128)}), f32[16,64,64]{1,2,0:T(8,128)}) %all-reduce.2.cloned.1.call-update) | async-done | bytes 262160 | tf_op jit(solution)/shard_map/psum | solution.py:94
  116.0 2.8 %fusion.27 = f32[16,64,64]{1,2,0:T(8,128)S(1)} fusion(f32[16,64,64]{1,2,0:T(8,128)} %all-reduce.2.cloned.1.call-done, f32[64]{0:T(128)S(1)} %get-tuple-element.232, f32[64]{0:T(128)S(1)} %get-tuple-element.231), kind=kOutput, calls=%fused_computation.47 | convolution fusion | flops 50343936 | bytes 524800 | tf_op jit(solution)/shard_map/kn,ckl,lm->cnm/dot_general | solution.py:30
  118.8 0.8 multiply_reduce_fusion
  119.7 0.3 copy.29
  120.1 0.9 reshape.224
  (171 shorter events, 10.9 us)
Async XLA Ops:
  7.2 108.9 %all-reduce.2.cloned.1.call-start = ((), (), s32[]{:S(2)}) async-start(), calls=%async_computation | async-start | bytes 1048576 | tf_op jit(solution)/shard_map/psum | solution.py:94
  7.2 0.8 copy-start
Sparse Core Ops, SparseCore 0:
  60.1 55.8 all-reduce.1
where the time goes:
time: 128 us
  waiting for transfers between devices  39.8 us (31%)
  blocking collectives  28 us (22%)
  local copies, waits for them, and re-layouts  24.9 us (19%)
  matrix products  15.8 us (12%)
  between operations  14.2 us (11%)
  other arithmetic  3.41 us (3%)
  loops' own time  1.61 us (1%)
    psum x1, waiting for transfers between devices, shards(): totals = lax.psum(partial_sum, 'node')  39.7 us
    all_gather x1, blocking collectives, shards(): lax.all_gather(indices, 'chip', axis=0, tiled=True)  14.8 us
    all_gather x1, blocking collectives, shards(): lax.all_gather(picked[None], 'chip', axis=0, tiled=True)  13.2 us
    dynamic_update_slice x32, local copies, waits for them, and re-layouts, decode_block(): return lax.map(one_span, (values_rows, slot_rows))  12.6 us
    dot_general x32, matrix products, one_span(): lax.dot_general(left_hot, right_hot, (((0,), (0,)), ((), ())), preferred_...  8.39 us
    gather x4, local copies, waits for them, and re-layouts, shards(): picked = jnp.take_along_axis(coeffs, slots, axis=1).astype(jnp.bfloat16)  5.09 us
    dot_general x4, matrix products, inverse_blocks(): jnp.einsum('kn,ckl,lm->cnm', cosines, blocks, cosines, precision=lax.Prec...  5.02 us
    broadcast_in_dim x32, local copies, waits for them, and re-layouts, decode_block(): return lax.map(one_span, (values_rows, slot_rows))  2.91 us
  transfers between devices with their start and end apart: 1, of which 1 were waited for; matrix products, arithmetic and copies ran while one was open for 12% of the time, Pallas kernels for 0%

commit v1 on v0

--- a/solution.py
+++ b/solution.py
@@ -91,7 +91,9 @@
         lax.all_gather(picked[None], "chip", axis=0, tiled=True),
         lax.all_gather(indices, "chip", axis=0, tiled=True),
     )
-    totals = lax.psum(partial_sum, "node")
+    totals = partial_sum
+    for hop in (1, 2, 4):
+        totals = totals + lax.ppermute(totals, "node", [(dev, dev ^ hop) for dev in range(8)])
     update = place_blocks(
         normalized(inverse_blocks(totals, cosines, SPAN)), row_count, col_count, SPAN
     )

time: 128 us -> 80.4 us (0.63)
  waiting for transfers between devices: 39.8 us -> 5.33 us
  between operations: 14.2 us -> 0.81 us
  starting transfers between devices: 0.04 us -> 3.21 us
  matrix products: 15.8 us -> 13.7 us
    psum x1 -> x0, waiting for transfers between devices: 39.7 us -> none  [shards(): totals = lax.psum(partial_sum, 'node')]
    ppermute x0 -> x3, waiting for transfers between devices: none -> 5.33 us  [shards(): lax.ppermute(totals, 'node', [(dev, dev ^ hop) for dev in range(8)])]
    ppermute x0 -> x3, starting transfers between devices: none -> 3.21 us  [shards(): lax.ppermute(totals, 'node', [(dev, dev ^ hop) for dev in range(8)])]
    dot_general x4, matrix products: 5.02 us -> 2.97 us  [inverse_blocks(): jnp.einsum('kn,ckl,lm->cnm', cosines, blocks, cosines, precision=lax.Prec...]
  transfers between devices with their start and end apart: 1 -> 3, of which waited for: 1 -> 2; matrix products, arithmetic and copies ran while one was open for 12% -> 19% of each run, Pallas kernels for 0% -> 0%
where the time goes in v1:
time: 80.4 us; the launch traced here: 80.2 us
  blocking collectives  28.1 us (35%)
  local copies, waits for them, and re-layouts  23.9 us (30%)
  matrix products  13.7 us (17%)
  waiting for transfers between devices  5.33 us (7%)
  other arithmetic  3.49 us (4%)
  starting transfers between devices  3.21 us (4%)
  loops' own time  1.61 us (2%)
  between operations  0.81 us (1%)
    all_gather x1, blocking collectives, shards(): lax.all_gather(indices, 'chip', axis=0, tiled=True)  14.8 us
    all_gather x1, blocking collectives, shards(): lax.all_gather(picked[None], 'chip', axis=0, tiled=True)  13.2 us
    dynamic_update_slice x32, local copies, waits for them, and re-layouts, decode_block(): return lax.map(one_span, (values_rows, slot_rows))  12.6 us
    dot_general x32, matrix products, one_span(): lax.dot_general(left_hot, right_hot, (((0,), (0,)), ((), ())), preferred_...  8.39 us
    ppermute x3, waiting for transfers between devices, shards(): lax.ppermute(totals, 'node', [(dev, dev ^ hop) for dev in range(8)])  5.33 us
    gather x4, local copies, waits for them, and re-layouts, shards(): picked = jnp.take_along_axis(coeffs, slots, axis=1).astype(jnp.bfloat16)  5.09 us
    ppermute x3, starting transfers between devices, shards(): lax.ppermute(totals, 'node', [(dev, dev ^ hop) for dev in range(8)])  3.21 us
    dot_general x4, matrix products, inverse_blocks(): jnp.einsum('kn,ckl,lm->cnm', cosines, blocks, cosines, precision=lax.Prec...  2.97 us
  transfers between devices with their start and end apart: 3, of which 2 were waited for; matrix products, arithmetic and copies ran while one was open for 19% of the time, Pallas kernels for 0%

profile of v1, /device:TPU:0, one launch (start us, length us, event | category | flops | bytes accessed | tf_op | source)
XLA Modules:
  0.0 80.2 jit_solution(8720779034838987607)
XLA Ops:
  0.7 0.8 fusion.53
  1.4 14.8 %all_gather.6 = s32[4,16,32]{2,1,0:T(8,128)S(1)} all-gather(s32[1,16,32]{2,1,0:T(8,128)S(1)} %copy-done), channel_id=1, replica_groups=mesh['node'=8,'chip'=4] {'chip'}, dimensions={0}, use_global_device_ids=true | all-gather | bytes 10240 | tf_op jit(solution)/shard_map/all_gather | solution.py:92
  16.3 1.1 %convert_add_fusion = f32[1,128,512]{2,1,0:T(8,128)S(1)} fusion(bf16[1,128,512]{2,1,0:T(8,128)(2,1)} %param.8, f32[1,128,512]{2,1,0:T(8,128)} %param.7), kind=kLoop, calls=%fused_computation.41 | loop fusion | flops 196608 | bytes 655360 | tf_op jit(solution)/shard_map/add | solution.py:82
  17.7 1.7 %fusion.20 = f32[2,8,64,64]{2,3,1,0:T(8,128)S(1)} fusion(f32[2,64,8,64]{1,3,2,0:T(8,128)S(1)} %copy.21, f32[64]{0:T(128)S(1)} %get-tuple-element.232, f32[64]{0:T(128)S(1)} %get-tuple-element.231), kind=kOutput, calls=%fused_computation.37 | convolution fusion | flops 50343936 | bytes 524800 | tf_op jit(solution)/shard_map/kn,abnm,lm->abkl/dot_general | solution.py:22
  19.4 0.7 fusion.22
  20.1 0.3 reshape.216
  20.4 4.8 %gather_fusion = bf16[512]{0:T(512)(128)(2,1)S(1)} fusion(bf16[16,4096]{1,0:T(8,128)(2,1)S(1)} %reshape.216, s32[512]{0:T(512)S(1)} %reshape.225), kind=kCustom, calls=%fused_computation | custom fusion | bytes 6144 | tf_op jit(solution)/shard_map/jit(take_along_axis)/gather | solution.py:85
  25.4 13.2 %all_gather.7 = bf16[4,16,32]{2,1,0:T(8,128)(2,1)S(1)} all-gather(bf16[1,16,32]{2,1,0:T(8,128)(2,1)S(1)} %select_convert_fusion), channel_id=1, replica_groups=mesh['node'=8,'chip'=4] {'chip'}, dimensions={0}, use_global_device_ids=true | all-gather | bytes 5120 | tf_op jit(solution)/shard_map/all_gather | solution.py:91
  38.8 13.3 %while.37 = (s32[]{:T(128)}, f32[16,4096]{1,0:T(8,128)S(1)}, s32[16,128]{1,0:T(8,128)S(1)}, bf16[16,128]{1,0:T(8,128)(2,1)S(1)}, s32[]{:T(128)}, /*index=5*/s32[]{:T(128)}) while((s32[]{:T(128)}, f32[16,4096]{1,0:T(8,128)S(1)}, s32[16,128]{1,0:T(8,128)S(1)}, bf16[16,128]{1,0:T(8,128)(2,1)S(1)}, s32[]{:T(128)}, ...), condition=%wide.region_3.4_spmd.clone.clone, body=%wide.region_2.3_spmd.clone.clone.sunk | while | flops 1075714 | bytes 86353 | solution.py:60
  38.9 0.3 fusion.72
  39.3 0.4 dynamic_update_slice.20
  39.7 0.3 fusion.72
  40.1 0.4 dynamic_update_slice.20
  40.6 0.3 fusion.72
  40.9 0.4 dynamic_update_slice.20
  41.4 0.3 fusion.72
  41.8 0.4 dynamic_update_slice.20
  42.2 0.3 fusion.72
  42.6 0.4 dynamic_update_slice.20
  43.1 0.3 fusion.72
  43.4 0.4 dynamic_update_slice.20
  43.9 0.3 fusion.72
  44.3 0.4 dynamic_update_slice.20
  44.7 0.3 fusion.72
  45.1 0.4 dynamic_update_slice.20
  45.6 0.3 fusion.72
  45.9 0.4 dynamic_update_slice.20
  46.8 0.4 dynamic_update_slice.20
  47.2 0.3 fusion.72
  47.6 0.4 dynamic_update_slice.20
  48.4 0.4 dynamic_update_slice.20
  49.2 0.4 dynamic_update_slice.20
  50.1 0.4 dynamic_update_slice.20
  50.9 0.4 dynamic_update_slice.20
  51.7 0.4 dynamic_update_slice.20
  52.3 1.4 %collective-permute-done = f32[16,4096]{1,0:T(8,128)S(1)} collective-permute-done((f32[16,4096]{1,0:T(8,128)S(1)}, f32[16,4096]{1,0:T(8,128)S(1)}, u32[]{:S(2)}, u32[]{:S(2)}) %collective-permute-start) | collective-permute-done | bytes 262176 | tf_op jit(solution)/shard_map/ppermute | solution.py:96
  53.8 1.6 %collective-permute-start.1 = (f32[16,4096]{1,0:T(8,128)S(1)}, f32[16,4096]{1,0:T(8,128)S(1)}, u32[]{:S(2)}, u32[]{:S(2)}) collective-permute-start(f32[16,4096]{1,0:T(8,128)S(1)} %add.144), channel_id=1, source_target_pairs={{0,8},{4,12},{8,0},{12,4},{16,24},{20,28},{24,16},{28,20},{1,9},{5... | collective-permute-start | bytes 786440 | tf_op jit(solution)/shard_map/ppermute | solution.py:96
  55.4 13.3 %while.36 = (s32[]{:T(128)}, f32[16,4096]{1,0:T(8,128)S(1)}, s32[16,32]{1,0:T(8,128)S(1)}, bf16[16,32]{1,0:T(8,128)(2,1)S(1)}, s32[]{:T(128)}, /*index=5*/s32[]{:T(128)}) while((s32[]{:T(128)}, f32[16,4096]{1,0:T(8,128)S(1)}, s32[16,32]{1,0:T(8,128)S(1)}, bf16[16,32]{1,0:T(8,128)(2,1)S(1)}, s32[]{:T(128)}, ...), condition=%wide.region_1.2_spmd.clone.clone, body=%wide.region_0.1_spmd.clone.clone.sunk | while | flops 268930 | bytes 83089 | solution.py:60
  55.8 0.4 dynamic_update_slice.19
  56.6 0.4 dynamic_update_slice.19
  57.5 0.4 dynamic_update_slice.19
  58.3 0.4 dynamic_update_slice.19
  59.1 0.4 dynamic_update_slice.19
  59.9 0.4 dynamic_update_slice.19
  60.8 0.4 dynamic_update_slice.19
  61.6 0.4 dynamic_update_slice.19
  62.4 0.4 dynamic_update_slice.19
  63.3 0.4 dynamic_update_slice.19
  64.1 0.4 dynamic_update_slice.19
  64.9 0.4 dynamic_update_slice.19
  65.8 0.4 dynamic_update_slice.19
  66.6 0.4 dynamic_update_slice.19
  67.4 0.4 dynamic_update_slice.19
  68.3 0.4 dynamic_update_slice.19
  68.9 1.6 %collective-permute-start.2 = (f32[16,4096]{1,0:T(8,128)S(1)}, f32[16,4096]{1,0:T(8,128)S(1)}, u32[]{:S(2)}, u32[]{:S(2)}) collective-permute-start(f32[16,4096]{1,0:T(8,128)S(1)} %add.145), channel_id=1, source_target_pairs={{0,16},{4,20},{8,24},{12,28},{16,0},{20,4},{24,8},{28,12},{1,17},{... | collective-permute-start | bytes 786440 | tf_op jit(solution)/shard_map/ppermute | solution.py:96
  70.5 0.7 fusion.31
  71.3 0.7 fusion.29
  72.0 0.3 copy.25
  72.4 0.7 sub.16
  73.2 3.9 %collective-permute-done.2 = f32[16,4096]{1,0:T(8,128)S(1)} collective-permute-done((f32[16,4096]{1,0:T(8,128)S(1)}, f32[16,4096]{1,0:T(8,128)S(1)}, u32[]{:S(2)}, u32[]{:S(2)}) %collective-permute-start.2) | collective-permute-done | bytes 262176 | tf_op jit(solution)/shard_map/ppermute | solution.py:96
  77.3 0.7 fusion.27
  78.1 0.8 multiply_reduce_fusion
  79.0 0.3 copy.30
  79.3 0.9 %reshape.224 = f32[128,512]{1,0:T(8,128)} reshape(f32[2,64,8,64]{3,2,1,0:T(8,128)S(1)} %copy.30) | data formatting | bytes 524288 | tf_op jit(solution)/shard_map/reshape | solution.py:35
  (176 shorter events, 11.5 us)
Async XLA Ops:
  0.6 0.8 copy-start
  52.2 1.6 %collective-permute-start = (f32[16,4096]{1,0:T(8,128)S(1)}, f32[16,4096]{1,0:T(8,128)S(1)}, u32[]{:S(2)}, u32[]{:S(2)}) collective-permute-start(f32[16,4096]{1,0:T(8,128)S(1)} %get-tuple-element.160), channel_id=1, source_target_pairs={{0,4},{4,0},{8,12},{12,8},{16,20},{20,16},{24,28},{28,24},{1,5},{5... | collective-permute-start | bytes 786440 | tf_op jit(solution)/shard_map/ppermute | solution.py:96
  53.8 15.1 %collective-permute-start.1 = (f32[16,4096]{1,0:T(8,128)S(1)}, f32[16,4096]{1,0:T(8,128)S(1)}, u32[]{:S(2)}, u32[]{:S(2)}) collective-permute-start(f32[16,4096]{1,0:T(8,128)S(1)} %add.144), channel_id=1, source_target_pairs={{0,8},{4,12},{8,0},{12,4},{16,24},{20,28},{24,16},{28,20},{1,9},{5... | collective-permute-start | bytes 786440 | tf_op jit(solution)/shard_map/ppermute | solution.py:96
  68.9 8.1 %collective-permute-start.2 = (f32[16,4096]{1,0:T(8,128)S(1)}, f32[16,4096]{1,0:T(8,128)S(1)}, u32[]{:S(2)}, u32[]{:S(2)}) collective-permute-start(f32[16,4096]{1,0:T(8,128)S(1)} %add.145), channel_id=1, source_target_pairs={{0,16},{4,20},{8,24},{12,28},{16,0},{20,4},{24,8},{28,12},{1,17},{... | collective-permute-start | bytes 786440 | tf_op jit(solution)/shard_map/ppermute | solution.py:96
